TPU v7x, 32 devices: a whole 2x2x4 slice. The times are simulated.
32 devices in a mesh: gx: 2 (over x), gy: 4 (over z), wa: 4 (over y, core).
Axes of the slice: x: 2, y: 2, z: 4, core: 2. Of those that a mesh axis runs over, the one named last changes fastest.
Arguments:
- velocity: float32 [3, 64, 256, 512], P(None, 'gx', 'gy', 'wa'), may hold values from -70 to 70, as said below
- lengths: int32 [2, 4, 4, 2048], P('gx', 'gy', 'wa'), may hold values from 16 to 128
- destinations: int32 [2, 4, 4, 2048, 1], P('gx', 'gy', 'wa'), may hold values from 0 to 7; in each aligned block of 2048 rows (0 to 2047, 2048 to 4095, ..., all dimensions but the last counted through in order) at most 512 rows name the same one
Outputs:
- received: float32 [8, 4, 3, 8, 512, 128], P(('gx', 'gy'), 'wa')
Inputs may be any that keep to these rules, and one draw needn't show every extreme that they name: `velocity`: finite values; the amplitude varies over the grid. `destinations`: in every draw no device sends more than 512 blocks to one writer, and some device sends exactly 512 to one writer.
All inputs are finite; a program needn't handle non-finite values.
Results may differ from a plain program's by a relative error of at most 0.0003.
Values sent between devices are 32-bit elements; how exact they have to be, the bound alone decides.
A program may use at most 128 MiB of HBM per device.

v0:
```python
import jax
import jax.numpy as jnp
from jax import lax
from jax.sharding import PartitionSpec as P

BY = 8
BZ = 16


def extended(array, sides, width):
    for axis, dim in sides:
        peers, length = (lax.axis_size(axis), array.shape[dim])
        up = [(i, (i + 1) % peers) for i in range(peers)]
        down = [(j, i) for i, j in up]
        last = lax.slice_in_dim(array, length - width, length, axis=dim)
        leading = lax.slice_in_dim(array, 0, width, axis=dim)
        before = lax.ppermute(last, axis, up)
        after = lax.ppermute(leading, axis, down)
        array = jnp.concatenate([before, array, after], axis=dim)
    return array


def dct_table(count):
    freqs = jnp.arange(count, dtype=jnp.float32)[:, None]
    points = jnp.arange(count, dtype=jnp.float32)[None, :]
    table = jnp.cos(jnp.pi * (points + 0.5) * freqs / count) * jnp.sqrt(2.0 / count)
    return jnp.where(freqs == 0.0, table * jnp.sqrt(0.5), table)


def curl_field(padded):

    def along_x(component):
        return (padded[component, 2:, 1:-1, 1:-1] - padded[component, :-2, 1:-1, 1:-1]) * 0.5

    def along_y(component):
        return (padded[component, 1:-1, 2:, 1:-1] - padded[component, 1:-1, :-2, 1:-1]) * 0.5

    def along_z(component):
        return (padded[component, 1:-1, 1:-1, 2:] - padded[component, 1:-1, 1:-1, :-2]) * 0.5

    first = along_y(2) - along_z(1)
    second = along_z(0) - along_x(2)
    third = along_x(1) - along_y(0)
    return jnp.stack([first, second, third])


def transform(curl):
    comps, cells_x, cells_y, cells_z = curl.shape
    kron_table = jnp.kron(dct_table(BY), dct_table(BZ)).T.reshape(BY, BZ, BY * BZ)
    grouped = curl.reshape(comps, cells_x, cells_y // BY, BY, cells_z // BZ, BZ)
    coeffs = lax.dot_general(
        grouped,
        kron_table,
        (((3, 5), (0, 1)), ((), ())),
        precision=lax.Precision.HIGHEST,
        preferred_element_type=jnp.float32,
    )
    return coeffs.reshape(comps, -1, BY * BZ)


def local(velocity, lengths, destinations):
    padded = extended(velocity, (("gx", 1), ("gy", 2), ("wa", 3)), 1)
    curl = curl_field(padded)
    coeffs = transform(curl)
    total = lax.psum(jnp.sum(coeffs * coeffs), ("gx", "gy", "wa"))
    every = curl.size * lax.axis_size("gx") * lax.axis_size("gy") * lax.axis_size("wa")
    rms = jnp.sqrt(total / every + 1e-06)
    comps, nblk, width = coeffs.shape
    rows_x = lax.axis_size("gx")
    rows_y = lax.axis_size("gy")
    writer_count = rows_x * rows_y
    capacity = max(2, 2 * nblk // writer_count)
    targets = destinations.reshape(nblk)
    lens = lengths.reshape(nblk)
    onehot = (targets[:, None] == jnp.arange(writer_count, dtype=jnp.int32)[None, :]).astype(
        jnp.int32
    )
    before = jnp.cumsum(onehot, axis=0) - onehot
    ranking = jnp.sum(before * onehot, axis=1)
    slot_index = targets * capacity + ranking
    source = jnp.full((writer_count * capacity,), -1, jnp.int32)
    source = source.at[slot_index].set(jnp.arange(nblk, dtype=jnp.int32))
    present = source >= 0
    safe = jnp.maximum(source, 0)
    picked = jnp.take(coeffs, safe, axis=1)
    freqs = jnp.arange(width, dtype=jnp.int32)
    keep = (freqs[None, :] < jnp.take(lens, safe)[:, None]) & present[:, None]
    outgoing = jnp.where(keep[None, :, :], picked / rms, 0.0)
    outgoing = outgoing.reshape(comps, writer_count, capacity, width)
    arrived = lax.all_to_all(outgoing, ("gx", "gy"), split_axis=1, concat_axis=1, tiled=True)
    return arrived.reshape(1, 1, comps, writer_count, capacity, width)


def solution(mesh):
    return jax.shard_map(
        local,
        mesh=mesh,
        in_specs=(
            P(None, "gx", "gy", "wa"),
            P("gx", "gy", "wa", None),
            P("gx", "gy", "wa", None, None),
        ),
        out_specs=P(("gx", "gy"), "wa", None, None, None, None),
        check_vma=False,
    )
```

profile of v0, /device:TPU:0, one launch (start us, length us, event | category | flops | bytes accessed | tf_op | source)
XLA Modules:
  0.0 421.0 jit_solution(12236084759855769985)
XLA Ops:
  1.0 3.0 collective-permute-start
  9.1 8.1 %scatter_custom_fusion = s32[4096]{0:T(1024)S(1)} fusion(s32[2048]{0:T(1024)S(1)} %bitcast.65, s32[2048]{0:T(1024)S(1)} %iota.50, s32[]{:T(128)} %constant.22.clone.1), kind=kCustom, calls=%fused_computation.49 | custom fusion | bytes 16388 | tf_op jit(solution)/shard_map/scatter | solution.py:82
  17.2 23.0 %gather_fusion = s32[4096]{0:T(1024)S(1)} fusion(s32[2048]{0:T(1024)S(1)} %bitcast.53, s32[4096]{0:T(1024)S(1)} %maximum_clamp_fusion), kind=kCustom, calls=%fused_computation | custom fusion | bytes 49152 | tf_op jit(solution)/shard_map/jit(_take)/gather | solution.py:87
  44.2 2.8 constant_dynamic-update-slice_fusion.5
  48.7 4.1 collective-permute-start.2
  55.7 3.6 copy.36
  59.3 3.7 copy.37
  63.1 3.7 copy.38
  66.8 3.8 copy.39
  73.0 10.2 %copy.19 = f32[3,34,66,128]{1,3,2,0:T(8,128)} copy(f32[3,34,66,128]{3,2,1,0:T(8,128)} %pad_maximum_fusion.2) | data formatting | bytes 6893568 | tf_op jit(solution)/shard_map/concatenate | solution.py:19
  88.2 3.8 copy.40
  94.6 10.3 %multiply_subtract_fusion = f32[1,32,64,128]{1,3,2,0:T(8,128)} fusion(f32[1,32,64,128]{1,3,2,0:T(8,128)} %copy.40, f32[1,32,64,128]{1,3,2,0:T(8,128)} %copy.41, f32[1,32,64,128]{1,3,2,0:T(8,128)} %copy.38, f32[1,32,64,128]{1,3,2,0:T(8,128)} %copy.39), kind=kLoop, calls=%fused_computation.15 | loop fusion | flops 1310720 | bytes 5242880 | tf_op jit(solution)/shard_map/sub | solution.py:43
  105.0 2.7 copy.34
  107.7 2.8 copy.35
  110.5 18.6 %fusion.6 = (f32[1,32,64,128]{1,3,2,0:T(8,128)}, f32[1,32,64,128]{1,3,2,0:T(8,128)}) fusion(f32[3,34,66,128]{1,3,2,0:T(8,128)} %copy.19, f32[3,34,66,1]{1,3,2,0:T(1,128)} %collective-permute-done.5, f32[3,34,66,1]{1,3,2,0:T(1,128)} %collective-permute-done.4, f32[1,32,64,128]{1,3,2,0:T(8,128)} %copy.34, f32[1,32,64,128]{1,3,2,0:T(8,128)} %copy.35, ...), kind=kLoop, calls=%fused_computation.14 | loop fusion | flops 3670016 | bytes 9792096 | tf_op jit(solution)/shard_map/sub | solution.py:41
  129.2 10.3 %maximum_bitcast_fusion = f32[3,32,8,8,8,16]{1,5,3,4,2,0:T(8,128)} fusion(f32[1,32,8,8,8,16]{1,5,4,3,2,0:T(8,128)S(1)} %bitcast.57, f32[1,32,8,8,8,16]{1,5,4,3,2,0:T(8,128)} %bitcast.59, f32[1,32,8,8,8,16]{1,5,4,3,2,0:T(8,128)} %bitcast.58), kind=kLoop, calls=%fused_computation.3 | loop fusion | flops 1572864 | bytes 6291456 | tf_op jit(solution)/shard_map/dot_general | solution.py:51
  139.5 23.0 %copy.42 = f32[3,32,8,8,8,16]{5,3,2,1,4,0:T(8,128)} copy(f32[3,32,8,8,8,16]{1,5,3,4,2,0:T(8,128)} %maximum_bitcast_fusion) | data formatting | bytes 6291456 | tf_op jit(solution)/shard_map/dot_general | solution.py:51
  162.5 24.0 %multiply_reduce_fusion = (f32[]{:T(128)}, f32[3,2048,128]{2,1,0:T(8,128)S(1)}) fusion(f32[3,2048,8,16]{3,1,2,0:T(8,128)} %bitcast.54, f32[8,16,128,1]{2,1,0,3:T(8,128)S(1)} %bitcast.60), kind=kOutput, calls=%fused_computation.17 | convolution fusion | flops 1209532416 | bytes 6356996 | tf_op jit(solution)/shard_map/dot_general | solution.py:51
  186.5 10.0 %copy.30 = f32[3,2048,128]{2,0,1:T(4,128)} copy(f32[3,2048,128]{2,1,0:T(8,128)S(1)} %get-tuple-element.33) | data formatting | bytes 6291456 | tf_op jit(solution)/shard_map/dot_general | solution.py:51
  196.4 32.3 %gather_fusion.1 = f32[4096,3,128]{2,1,0:T(4,128)} fusion(f32[3,2048,128]{2,0,1:T(4,128)} %copy.30, s32[4096]{0:T(1024)S(1)} %maximum_clamp_fusion), kind=kCustom, calls=%fused_computation.1 | custom fusion | bytes 12599296 | tf_op jit(solution)/shard_map/jit(_take)/gather | solution.py:85
  228.7 40.2 %psum.7 = f32[]{:T(128)} all-reduce(f32[]{:T(128)} %get-tuple-element.32), channel_id=1, replica_groups=mesh['gx'=2,'gy'=4,'wa'=4] {'gx','gy','wa'}, use_global_device_ids=true, to_apply=%region_5.6 | all-reduce | flops 1 | bytes 8 | tf_op jit(solution)/shard_map/psum | solution.py:65
  269.7 5.0 %fusion.1 = f32[3,8,512,128]{3,2,0,1:T(8,128)S(1)} fusion(f32[3,8,512,128]{3,0,2,1:T(4,128)} %bitcast.55, f32[]{:T(128)S(6)} %sqrt.3, pred[8,512]{1,0:T(8,128)(4,1)S(1)} %broadcast_in_dim.69, pred[8,512,128]{2,1,0:T(8,128)(4,1)S(1)} %copy-done.6), kind=kLoop, calls=%fused_computation.6 | loop fusion | flops 4718592 | bytes 13111300 | tf_op jit(solution)/shard_map/jit(_where)/select_n | solution.py:88
  274.7 143.2 %all_to_all.5 = f32[3,8,512,128]{3,2,0,1:T(8,128)S(1)} all-to-all(f32[3,8,512,128]{3,2,0,1:T(8,128)S(1)} %fusion.1), channel_id=1, replica_groups=mesh['gx'=2,'gy'=4,'wa'=4] {'gx','gy'}, dimensions={1} | all-to-all | bytes 12582912 | tf_op jit(solution)/shard_map/all_to_all | solution.py:90
  417.9 3.1 copy.32
  (57 shorter events, 24.7 us)
Async XLA Ops:
  0.0 17.2 %copy-start = (s32[1,1,1,2048]{3,2,1,0:T(1,128)S(1)}, s32[1,1,1,2048]{3,2,1,0:T(1,128)}, u32[]{:S(2)}) copy-start(s32[1,1,1,2048]{3,2,1,0:T(1,128)} %param.4) | copy-start | bytes 24580
  1.0 42.3 %collective-permute-start = (f32[3,1,64,128]{3,2,1,0:T(8,128)S(1)}, f32[3,1,64,128]{3,2,1,0:T(8,128)}, u32[]{:S(2)}, u32[]{:S(2)}) collective-permute-start(f32[3,1,64,128]{3,2,1,0:T(8,128)S(1)} %get-tuple-element.27), channel_id=1, source_target_pairs={{0,16},{16,0},{1,17},{17,1},{2,18},{18,2},{3,19},{19,3},{4,20},{20... | collective-permute-start | bytes 294920 | tf_op jit(solution)/shard_map/ppermute | solution.py:17
  4.0 43.0 %collective-permute-start.1 = (f32[3,1,64,128]{3,2,1,0:T(8,128)S(1)}, f32[3,1,64,128]{3,2,1,0:T(8,128)}, u32[]{:S(2)}, u32[]{:S(2)}) collective-permute-start(f32[3,1,64,128]{3,2,1,0:T(8,128)S(1)} %get-tuple-element.26), channel_id=1, source_target_pairs={{16,0},{0,16},{17,1},{1,17},{18,2},{2,18},{19,3},{3,19},{20,4},{4,... | collective-permute-start | bytes 294920 | tf_op jit(solution)/shard_map/ppermute | solution.py:18
  48.7 21.8 %collective-permute-start.2 = (f32[3,34,1,128]{3,2,1,0:T(1,128)}, f32[3,34,1,128]{3,2,1,0:T(1,128)S(1)}, u32[]{:S(2)}, u32[]{:S(2)}) collective-permute-start(f32[3,34,1,128]{3,2,1,0:T(1,128)} %get-tuple-element.18), channel_id=1, source_target_pairs={{4,0},{8,4},{12,8},{0,12},{5,1},{9,5},{13,9},{1,13},{6,2},{10,6},{... | collective-permute-start | bytes 156680 | tf_op jit(solution)/shard_map/ppermute | solution.py:18
  52.7 17.8 %collective-permute-start.3 = (f32[3,34,1,128]{3,2,1,0:T(1,128)}, f32[3,34,1,128]{3,2,1,0:T(1,128)S(1)}, u32[]{:S(2)}, u32[]{:S(2)}) collective-permute-start(f32[3,34,1,128]{3,2,1,0:T(1,128)} %get-tuple-element.17), channel_id=1, source_target_pairs={{0,4},{4,8},{8,12},{12,0},{1,5},{5,9},{9,13},{13,1},{2,6},{6,10},{... | collective-permute-start | bytes 156680 | tf_op jit(solution)/shard_map/ppermute | solution.py:17
  85.4 25.1 %collective-permute-start.4 = (f32[3,34,66,1]{1,3,2,0:T(1,128)}, f32[3,34,66,1]{1,3,2,0:T(1,128)}, u32[]{:S(2)}, u32[]{:S(2)}) collective-permute-start(f32[3,34,66,1]{1,3,2,0:T(1,128)} %get-tuple-element.9), channel_id=1, source_target_pairs={{1,0},{2,1},{3,2},{0,3},{5,4},{6,5},{7,6},{4,7},{9,8},{10,9},{11,1... | collective-permute-start | bytes 80792 | tf_op jit(solution)/shard_map/ppermute | solution.py:18
  85.5 25.0 %collective-permute-start.5 = (f32[3,34,66,1]{1,3,2,0:T(1,128)}, f32[3,34,66,1]{1,3,2,0:T(1,128)}, u32[]{:S(2)}, u32[]{:S(2)}) collective-permute-start(f32[3,34,66,1]{1,3,2,0:T(1,128)} %get-tuple-element.10), channel_id=1, source_target_pairs={{0,1},{1,2},{2,3},{3,0},{4,5},{5,6},{6,7},{7,4},{8,9},{9,10},{10,1... | collective-permute-start | bytes 80792 | tf_op jit(solution)/shard_map/ppermute | solution.py:17
  88.2 3.8 copy-start.5
  94.6 10.3 %copy-start.4 = (f32[1,32,64,128]{3,2,1,0:T(8,128)S(1)}, f32[1,32,64,128]{3,2,1,0:T(8,128)}, u32[]{:S(2)}) copy-start(f32[1,32,64,128]{3,2,1,0:T(8,128)} %get-tuple-element.16) | copy-start | bytes 3145732
  105.0 2.7 copy-start.3
  110.5 18.7 %copy-start.2 = (f32[1,32,64,128]{1,3,2,0:T(8,128)S(1)}, f32[1,32,64,128]{1,3,2,0:T(8,128)}, u32[]{:S(2)}) copy-start(f32[1,32,64,128]{1,3,2,0:T(8,128)} %multiply_subtract_fusion) | copy-start | bytes 3145732
  196.4 73.2 %copy-start.6 = (pred[8,512,128]{2,1,0:T(8,128)(4,1)S(1)}, pred[8,512,128]{2,1,0:T(8,128)(4,1)}, u32[]{:S(2)}) copy-start(pred[8,512,128]{2,1,0:T(8,128)(4,1)} %fusion.7) | copy-start | bytes 1572868
  417.9 3.1 copy-start.1
where the time goes:
time: 422 us; the launch traced here: 421 us
  blocking collectives  183 us (43%)
  local copies, waits for them, and re-layouts  149 us (35%)
  other arithmetic  56.5 us (13%)
  matrix products  24 us (6%)
  starting transfers between devices  7.68 us (2%)
    all_to_all x1, blocking collectives, local(): lax.all_to_all(outgoing, ('gx', 'gy'), split_axis=1, concat_axis=1, tiled...  143 us
    psum x1, blocking collectives, local(): total = lax.psum(jnp.sum(coeffs * coeffs), ('gx', 'gy', 'wa'))  40.2 us
    dot_general x2, local copies, waits for them, and re-layouts, transform(): lax.dot_general(grouped, kron_table, (((3, 5), (0, 1)), ((), ())), precis...  33 us
    gather x1, local copies, waits for them, and re-layouts, local(): picked = jnp.take(coeffs, safe, axis=1)  32.3 us
    unnamed x23, local copies, waits for them, and re-layouts  27.7 us
    dot_general x1, matrix products, transform(): lax.dot_general(grouped, kron_table, (((3, 5), (0, 1)), ((), ())), precis...  24 us
    gather x1, local copies, waits for them, and re-layouts, local(): keep = (freqs[None, :] < jnp.take(lens, safe)[:, None]) & present[:, None]  23 us
    sub x1, other arithmetic, curl_field(): first = along_y(2) - along_z(1)  18.6 us
  transfers between devices with their start and end apart: 6, of which 0 were waited for; matrix products, arithmetic and copies ran while one was open for 20% of the time, Pallas kernels for 0%

commit v1 on v0

v1 whole, which is shorter than its diff:
```python
import functools

import jax
import jax.numpy as jnp
import numpy as np
from jax import lax
from jax.experimental import pallas as pl
from jax.experimental.pallas import tpu as pltpu
from jax.sharding import PartitionSpec as P

BY = 8
BZ = 16
MESH = pl.DeviceIdType.MESH


def dct_table(count):
    freqs, points = np.arange(count)[:, None], np.arange(count)[None, :]
    table = np.cos(np.pi * (points + 0.5) * freqs / count) * np.sqrt(2.0 / count)
    return np.where(freqs == 0, table * np.sqrt(0.5), table)


def split_table():
    kron = np.kron(dct_table(BY), dct_table(BZ)).T.astype(np.float32)
    high = kron.astype(jnp.bfloat16)
    low = (kron - high.astype(np.float32)).astype(jnp.bfloat16)
    return np.block([[high, low], [high, np.zeros_like(low)]]).astype(jnp.bfloat16)


def faces(array, axis):
    peers = lax.axis_size(axis)
    up = [(i, (i + 1) % peers) for i in range(peers)]
    down = [(j, i) for i, j in up]
    first, last = array
    return lax.ppermute(last, axis, up), lax.ppermute(first, axis, down)


def slot_kernel(writers, capacity, targets, slots):
    t = targets[...]
    rows, lanes = t.shape
    shape = (lanes, lanes)
    upper = (
        lax.broadcasted_iota(jnp.int32, shape, 0) < lax.broadcasted_iota(jnp.int32, shape, 1)
    ).astype(jnp.float32).astype(jnp.bfloat16)
    square = (rows, rows)
    lower = (
        lax.broadcasted_iota(jnp.int32, square, 1) < lax.broadcasted_iota(jnp.int32, square, 0)
    ).astype(jnp.float32).astype(jnp.bfloat16)

    def body(w, acc):
        mine = t == w
        ones = mine.astype(jnp.float32).astype(jnp.bfloat16)
        inner = jnp.dot(ones, upper, preferred_element_type=jnp.float32)
        before = jnp.dot(lower, ones, preferred_element_type=jnp.float32)
        rank = inner + jnp.sum(before, axis=1, keepdims=True)
        return jnp.where(mine, w * capacity + rank.astype(jnp.int32), acc)

    slots[...] = lax.fori_loop(0, writers, body, jnp.zeros_like(t))


def block_rows(plane):
    cells_y, cells_z = plane.shape
    tiles = plane.reshape(cells_y // BY, BY, cells_z)
    sub = lax.broadcasted_iota(jnp.int32, tiles.shape, 1)
    group = lax.broadcasted_iota(jnp.int32, tiles.shape, 2) // BZ
    k = 1
    while k < BY:
        s_bit, g_bit = (sub & k) != 0, (group & k) != 0
        fwd = pltpu.roll(pltpu.roll(tiles, BY - k, 1), k * BZ, 2)
        back = pltpu.roll(pltpu.roll(tiles, k, 1), cells_z - k * BZ, 2)
        tiles = jnp.where(s_bit == g_bit, tiles, jnp.where(g_bit, fwd, back))
        k *= 2
    return tiles.reshape(cells_y, cells_z)


def blocks_kernel(
    slots, lens, vel, xb, xa, yb, ya, zb, za, table, out, squares, coeffs
):
    comps, cells_x, cells_y, cells_z = vel.shape
    nblk = coeffs.shape[1]
    per_plane = nblk // cells_x
    rows = out.shape[0] // comps
    width = out.shape[1]
    row = lax.broadcasted_iota(jnp.int32, (cells_y, cells_z), 0)
    lane = lax.broadcasted_iota(jnp.int32, (cells_y, cells_z), 1)
    chunk = 128

    def clear(i, _):
        out[pl.ds(pl.multiple_of(i * chunk, chunk), chunk), :] = jnp.zeros(
            (chunk, width), jnp.float32
        )
        return 0

    lax.fori_loop(0, out.shape[0] // chunk, clear, 0)

    def plane(x, acc):
        u, v, w = vel[0, x], vel[1, x], vel[2, x]

        def along_x(comp):
            nxt = jnp.where(
                x == cells_x - 1, xa[comp - 1], vel[comp, jnp.minimum(x + 1, cells_x - 1)]
            )
            prv = jnp.where(x == 0, xb[comp - 1], vel[comp, jnp.maximum(x - 1, 0)])
            return (nxt - prv) * 0.5

        def along_y(f, face):
            nxt = jnp.where(
                row == cells_y - 1, ya[face, pl.ds(x, 1), :], pltpu.roll(f, cells_y - 1, 0)
            )
            prv = jnp.where(row == 0, yb[face, pl.ds(x, 1), :], pltpu.roll(f, 1, 0))
            return (nxt - prv) * 0.5

        def along_z(f, face):
            after = pltpu.roll(za[face], cells_z - 1 - x, 1)
            before = pltpu.roll(zb[face], lax.rem(cells_z - x, cells_z), 1)
            nxt = jnp.where(lane == cells_z - 1, after, pltpu.roll(f, cells_z - 1, 1))
            prv = jnp.where(lane == 0, before, pltpu.roll(f, 1, 1))
            return (nxt - prv) * 0.5

        curl = (
            along_y(w, 1) - along_z(v, 1),
            along_z(u, 0) - along_x(2),
            along_x(1) - along_y(u, 0),
        )
        for c in curl:
            acc = acc + jnp.sum((c * c).reshape(cells_y // 8, 8, cells_z), axis=0)
        flat = jnp.concatenate([block_rows(c) for c in curl], axis=0)
        high = flat.astype(jnp.bfloat16)
        low = (flat - high.astype(jnp.float32)).astype(jnp.bfloat16)
        both = jnp.dot(
            jnp.concatenate([high, low], axis=1), table[...], preferred_element_type=jnp.float32
        )
        result = both[:, :width] + both[:, width:]
        start = pl.multiple_of(x * per_plane, 8)
        for c in range(comps):
            coeffs[c, pl.ds(start, per_plane), :] = result[c * per_plane : (c + 1) * per_plane]
        return acc

    squares[...] = lax.fori_loop(0, cells_x, plane, jnp.zeros((8, cells_z), jnp.float32))
    freqs = lax.broadcasted_iota(jnp.int32, (1, width), 1)
    group = 8

    def place(j, _):
        for k in range(group):
            i = j * group + k
            slot, keep = slots[i], freqs < lens[i]
            for c in range(comps):
                out[pl.ds(c * rows + slot, 1), :] = jnp.where(
                    keep, coeffs[c, pl.ds(i, 1), :], 0.0
                )
        return 0

    lax.fori_loop(0, nblk // group, place, 0)


def exchange_kernel(n_x, n_y, send, recv, send_sem, recv_sem):
    a, b = lax.axis_index("gx"), lax.axis_index("gy")
    c = lax.axis_index("wa")
    me = a * n_y + b
    offsets = [(i, j) for i in range(n_x) for j in range(n_y) if i or j]
    offsets.sort(key=lambda o: (bool(o[0]) and bool(o[1]), min(o[1], n_y - o[1])))
    barrier = pltpu.get_barrier_semaphore()
    peers = [(lax.rem(a + i, n_x), lax.rem(b + j, n_y)) for i, j in offsets]
    for pa, pb in peers:
        pl.semaphore_signal(barrier, inc=1, device_id=(pa, pb, c), device_id_type=MESH)
    pl.semaphore_wait(barrier, len(peers))
    copies = []
    for k, (pa, pb) in enumerate(peers):
        copy = pltpu.make_async_remote_copy(
            src_ref=send.at[:, pa * n_y + pb],
            dst_ref=recv.at[:, me],
            send_sem=send_sem.at[k],
            recv_sem=recv_sem.at[k],
            device_id=(pa, pb, c),
            device_id_type=MESH,
        )
        copy.start()
        copies.append(copy)
    for copy in copies:
        copy.wait()


def scale_kernel(every, me, squares, recv, send, out):
    total = jnp.sum(squares[...], keepdims=True)
    scale = 1.0 / jnp.sqrt(total / every + 1e-06)
    own = pl.program_id(1) == me[0]

    @pl.when(own)
    def _():
        out[...] = send[...] * scale[None, None]

    @pl.when(jnp.logical_not(own))
    def _():
        out[...] = recv[...] * scale[None, None]


def local(velocity, lengths, destinations):
    n_x, n_y, n_z = lax.axis_size("gx"), lax.axis_size("gy"), lax.axis_size("wa")
    comps, cells_x, cells_y, cells_z = velocity.shape
    width = BY * BZ
    nblk = cells_x * cells_y * cells_z // width
    writers = n_x * n_y
    capacity = max(2, 2 * nblk // writers)
    f32 = jnp.float32

    vw, uw, uv = velocity[1:], velocity[::2], velocity[:2]
    xb, xa = faces((vw[:, 0], vw[:, -1]), "gx")
    yb, ya = faces((uw[:, :, 0], uw[:, :, -1]), "gy")

    def z_face(f):
        return jnp.pad(f.transpose(0, 2, 1), ((0, 0), (0, 0), (0, cells_z - cells_x)))

    zb, za = faces((z_face(uv[..., 0]), z_face(uv[..., -1])), "wa")

    slots = pl.pallas_call(
        functools.partial(slot_kernel, writers, capacity),
        out_shape=jax.ShapeDtypeStruct((nblk // 128, 128), jnp.int32),
        name="slots",
    )(destinations.reshape(nblk // 128, 128))

    table = jnp.asarray(split_table())
    smem = pl.BlockSpec(memory_space=pltpu.SMEM)
    vmem = pl.BlockSpec(memory_space=pltpu.VMEM)
    outgoing, squares = pl.pallas_call(
        blocks_kernel,
        out_shape=(
            jax.ShapeDtypeStruct((comps * writers * capacity, width), f32),
            jax.ShapeDtypeStruct((8, cells_z), f32),
        ),
        in_specs=[smem, smem] + [vmem] * 8,
        out_specs=(vmem, vmem),
        scratch_shapes=[pltpu.VMEM((comps, nblk, width), f32)],
        compiler_params=pltpu.CompilerParams(vmem_limit_bytes=48 * 2**20),
        name="blocks",
    )(slots.reshape(nblk), lengths.reshape(nblk), velocity, xb, xa, yb, ya, zb, za, table)
    outgoing = outgoing.reshape(comps, writers, capacity, width)

    anywhere = pl.BlockSpec(memory_space=pl.ANY)
    arrived = pl.pallas_call(
        functools.partial(exchange_kernel, n_x, n_y),
        out_shape=jax.ShapeDtypeStruct(outgoing.shape, f32),
        in_specs=[anywhere],
        out_specs=anywhere,
        scratch_shapes=[
            pltpu.SemaphoreType.DMA((writers - 1,)),
            pltpu.SemaphoreType.DMA((writers - 1,)),
        ],
        compiler_params=pltpu.CompilerParams(collective_id=0, has_side_effects=True),
        name="exchange",
    )(outgoing)

    squares = lax.psum(squares, ("gx", "gy", "wa"))
    every = velocity.size * n_x * n_y * n_z
    me = (lax.axis_index("gx") * n_y + lax.axis_index("gy")).astype(jnp.int32).reshape(1)
    block = (1, 1, capacity, width)
    received = pl.pallas_call(
        functools.partial(scale_kernel, float(every)),
        grid_spec=pltpu.PrefetchScalarGridSpec(
            num_scalar_prefetch=1,
            grid=(comps, writers),
            in_specs=[
                pl.BlockSpec((8, cells_z), lambda i, s, me: (0, 0)),
                pl.BlockSpec(block, lambda i, s, me: (i, s, 0, 0)),
                pl.BlockSpec(block, lambda i, s, me: (i, me[0], 0, 0)),
            ],
            out_specs=pl.BlockSpec(block, lambda i, s, me: (i, s, 0, 0)),
        ),
        out_shape=jax.ShapeDtypeStruct(outgoing.shape, f32),
        name="scale",
    )(me, squares, arrived, outgoing)
    return received.reshape(1, 1, comps, writers, capacity, width)


def solution(mesh):
    return jax.shard_map(
        local,
        mesh=mesh,
        in_specs=(
            P(None, "gx", "gy", "wa"),
            P("gx", "gy", "wa", None),
            P("gx", "gy", "wa", None, None),
        ),
        out_specs=P(("gx", "gy"), "wa", None, None, None, None),
        check_vma=False,
    )
```

time: 422 us -> 247 us (0.59)
  Pallas kernels: 0 us -> 183 us
  blocking collectives: 183 us -> 39.7 us
  local copies, waits for them, and re-layouts: 149 us -> 14 us
  other arithmetic: 56.5 us -> 0 us
  matrix products: 24 us -> 0 us
    pallas_call x0 -> x4, Pallas kernels: none -> 183 us  [the longest x1 139 us: local(): pl.pallas_call(functools.partial(exchange_kernel, n_x, n_y), out_shape=ja...]
    all_to_all x1 -> x0, blocking collectives: 143 us -> none  [local(): lax.all_to_all(outgoing, ('gx', 'gy'), split_axis=1, concat_axis=1, tiled...]
    gather x2 -> x0, local copies, waits for them, and re-layouts: 55.3 us -> none  [the longest x1 32.3 us: local(): picked = jnp.take(coeffs, safe, axis=1)]
    dot_general x2 -> x0, local copies, waits for them, and re-layouts: 33 us -> none  [transform(): lax.dot_general(grouped, kron_table, (((3, 5), (0, 1)), ((), ())), precis...]
    sub x2 -> x0, other arithmetic: 29 us -> none  [the longest x1 18.6 us: curl_field(): first = along_y(2) - along_z(1)]
    dot_general x1 -> x0, matrix products: 24 us -> none  [transform(): lax.dot_general(grouped, kron_table, (((3, 5), (0, 1)), ((), ())), precis...]
    unnamed x23 -> x10, local copies, waits for them, and re-layouts: 27.7 us -> 5.93 us
    concatenate x3 -> x0, local copies, waits for them, and re-layouts: 13.9 us -> none  [extended(): array = jnp.concatenate([before, array, after], axis=dim)]
  transfers between devices with their start and end apart: 6 -> 6, of which waited for: 0 -> 0; matrix products, arithmetic and copies ran while one was open for 20% -> 5% of each run, Pallas kernels for 0% -> 1%
where the time goes in v1:
time: 247 us; the launch traced here: 246 us
  Pallas kernels  183 us (74%)
  blocking collectives  39.7 us (16%)
  local copies, waits for them, and re-layouts  14 us (6%)
  starting transfers between devices  8.85 us (4%)
    pallas_call x1, Pallas kernels, local(): pl.pallas_call(functools.partial(exchange_kernel, n_x, n_y), out_shape=ja...  139 us
    psum x1, blocking collectives, local(): squares = lax.psum(squares, ('gx', 'gy', 'wa'))  39.7 us
    pallas_call x1, Pallas kernels, local(): pl.pallas_call(blocks_kernel, out_shape=(jax.ShapeDtypeStruct((comps * wr...  24.9 us
    pallas_call x1, Pallas kernels, local(): pl.pallas_call(functools.partial(scale_kernel, float(every)), grid_spec=p...  16.2 us
    ppermute x6, starting transfers between devices, faces(): return (lax.ppermute(last, axis, up), lax.ppermute(first, axis, down))  8.85 us
    unnamed x10, local copies, waits for them, and re-layouts  5.93 us
  transfers between devices with their start and end apart: 6, of which 0 were waited for; matrix products, arithmetic and copies ran while one was open for 5% of the time, Pallas kernels for 1%

profile of v1, /device:TPU:0, one launch (start us, length us, event | category | flops | bytes accessed | tf_op | source)
XLA Modules:
  0.0 246.1 jit_solution(711106341200880500)
XLA Ops:
  0.0 1.7 slice_bitcast_fusion
  1.7 3.0 %collective-permute-start.1 = (f32[2,64,128]{2,1,0:T(8,128)}, f32[2,64,128]{2,1,0:T(8,128)S(1)}, u32[]{:S(2)}, u32[]{:S(2)}) collective-permute-start(f32[2,64,128]{2,1,0:T(8,128)} %get-tuple-element.11), channel_id=1, source_target_pairs={{16,0},{0,16},{17,1},{1,17},{18,2},{2,18},{19,3},{3,19},{20,4},{4,... | collective-permute-start | bytes 196616 | tf_op jit(solution)/shard_map/ppermute | solution.py:34
  4.6 0.0 collective-permute-start
  4.7 1.7 slice.29
  6.4 0.7 fusion.1
  7.1 2.1 collective-permute-start.2
  9.2 2.8 %fusion = (f32[2,32,64,1]{3,2,1,0:T(8,128)}, f32[2,32,64,1]{3,2,1,0:T(8,128)}) fusion(f32[3,32,64,128]{3,2,1,0:T(8,128)S(1)} %copy-done), kind=kLoop, calls=%fused_computation.2 | loop fusion | bytes 65536 | tf_op jit(solution)/shard_map/slice | solution.py:212
  11.9 2.6 %copy.15 = f32[2,32,64,1]{1,2,0,3:T(8,128)S(1)} copy(f32[2,32,64,1]{3,2,1,0:T(8,128)} %get-tuple-element.10) | data formatting | bytes 32768
  14.6 0.6 pad.7
  15.2 0.0 collective-permute-start.4
  15.2 2.6 %copy.16 = f32[2,32,64,1]{1,2,0,3:T(8,128)S(1)} copy(f32[2,32,64,1]{3,2,1,0:T(8,128)} %get-tuple-element.9) | data formatting | bytes 32768
  17.8 0.6 pad.8
  18.4 1.7 collective-permute-start.5
  20.2 0.0 collective-permute-done.2.yb
  20.2 2.0 collective-permute-start.3
  22.2 2.9 %slots.1 = s32[16,128]{1,0:T(8,128)} custom-call(s32[16,128]{1,0:T(8,128)} %bitcast.33), custom_call_target="tpu_custom_call" | custom-call | tf_op jit(solution)/shard_map/slots/pallas_call | solution.py:214
  25.1 0.0 collective-permute-done.3.ya
  25.1 0.0 collective-permute-done.1.xa
  25.1 0.0 collective-permute-done.4.zb
  25.2 0.7 copy-done.2
  25.8 24.9 %blocks.1 = (f32[12288,128]{1,0:T(8,128)}, f32[8,128]{1,0:T(8,128)S(1)}) custom-call(s32[2048]{0:T(1024)S(1)} %bitcast.26, s32[2048]{0:T(1024)S(1)} %bitcast.27, f32[3,32,64,128]{3,2,1,0:T(8,128)S(1)} %copy-done, f32[2,64,128]{2,1,0:T(8,128)S(1)} %collective-permute-done.xb, f32[2,64,128]{2,1,0:T(8,128)S(1)} %collective-permute-done.1.xa, ...), custom_call_target="tpu_custom_call" | custom-call | tf_op jit(solution)/shard_map/blocks/pallas_call | solution.py:223
  50.7 39.7 %psum.7.squares = f32[8,128]{1,0:T(8,128)} all-reduce(f32[8,128]{1,0:T(8,128)S(1)} %get-tuple-element.7), channel_id=1, replica_groups=mesh['gx'=2,'gy'=4,'wa'=4] {'gx','gy','wa'}, use_global_device_ids=true, to_apply=%region_0.1 | all-reduce | flops 1024 | bytes 8192 | tf_op jit(solution)/shard_map/psum | solution.py:251
  90.4 139.5 %exchange.1.recv = f32[3,8,512,128]{3,2,1,0:T(8,128)} custom-call(f32[3,8,512,128]{3,2,1,0:T(8,128)} %bitcast.28), custom_call_target="tpu_custom_call" | custom-call | tf_op jit(solution)/shard_map/exchange/pallas_call | solution.py:238
  229.9 16.2 %scale.1 = f32[3,8,512,128]{3,2,1,0:T(8,128)} custom-call(s32[1]{0:T(128)} %bitcast.me, f32[8,128]{1,0:T(8,128)} %psum.7.squares, f32[3,8,512,128]{3,2,1,0:T(8,128)} %exchange.1.recv, f32[3,8,512,128]{3,2,1,0:T(8,128)} %bitcast.29), custom_call_target="tpu_custom_call" | custom-call | tf_op jit(solution)/shard_map/scale/pallas_call | solution.py:255
  (9 shorter events, 0.0 us)
Async XLA Ops:
  0.0 9.2 %copy-start = (f32[3,32,64,128]{3,2,1,0:T(8,128)S(1)}, f32[3,32,64,128]{3,2,1,0:T(8,128)}, u32[]{:S(2)}) copy-start(f32[3,32,64,128]{3,2,1,0:T(8,128)} %vel.1) | copy-start | bytes 9437188
  1.7 23.4 %collective-permute-start.1 = (f32[2,64,128]{2,1,0:T(8,128)}, f32[2,64,128]{2,1,0:T(8,128)S(1)}, u32[]{:S(2)}, u32[]{:S(2)}) collective-permute-start(f32[2,64,128]{2,1,0:T(8,128)} %get-tuple-element.11), channel_id=1, source_target_pairs={{16,0},{0,16},{17,1},{1,17},{18,2},{2,18},{19,3},{3,19},{20,4},{4,... | collective-permute-start | bytes 196616 | tf_op jit(solution)/shard_map/ppermute | solution.py:34
  4.6 20.4 %collective-permute-start = (f32[2,64,128]{2,1,0:T(8,128)}, f32[2,64,128]{2,1,0:T(8,128)S(1)}, u32[]{:S(2)}, u32[]{:S(2)}) collective-permute-start(f32[2,64,128]{2,1,0:T(8,128)} %get-tuple-element.12), channel_id=1, source_target_pairs={{0,16},{16,0},{1,17},{17,1},{2,18},{18,2},{3,19},{19,3},{4,20},{20... | collective-permute-start | bytes 196616 | tf_op jit(solution)/shard_map/ppermute | solution.py:34
  7.1 13.1 %collective-permute-start.2 = (f32[2,32,128]{2,1,0:T(8,128)}, f32[2,32,128]{2,1,0:T(8,128)}, u32[]{:S(2)}, u32[]{:S(2)}) collective-permute-start(f32[2,32,128]{2,1,0:T(8,128)} %bitcast.6), channel_id=1, source_target_pairs={{0,4},{4,8},{8,12},{12,0},{1,5},{5,9},{9,13},{13,1},{2,6},{6,10},{... | collective-permute-start | bytes 98312 | tf_op jit(solution)/shard_map/ppermute | solution.py:34
  11.9 13.2 %copy-start.1 = (bf16[256,256]{1,0:T(8,128)(2,1)S(1)}, bf16[256,256]{1,0:T(8,128)(2,1)}, u32[]{:S(2)}) copy-start(bf16[256,256]{1,0:T(8,128)(2,1)} %constant.18.clone.table) | copy-start | bytes 393220
  11.9 13.2 %copy-start.3 = (s32[1,1,1,2048]{3,2,1,0:T(1,128)S(1)}, s32[1,1,1,2048]{3,2,1,0:T(1,128)}, u32[]{:S(2)}) copy-start(s32[1,1,1,2048]{3,2,1,0:T(1,128)} %param.5) | copy-start | bytes 24580
  15.2 9.9 %collective-permute-start.4 = (f32[2,64,128]{2,1,0:T(8,128)}, f32[2,64,128]{2,1,0:T(8,128)S(1)}, u32[]{:S(2)}, u32[]{:S(2)}) collective-permute-start(f32[2,64,128]{2,1,0:T(8,128)} %pad.7), channel_id=1, source_target_pairs={{0,1},{1,2},{2,3},{3,0},{4,5},{5,6},{6,7},{7,4},{8,9},{9,10},{10,1... | collective-permute-start | bytes 196616 | tf_op jit(solution)/shard_map/ppermute | solution.py:34
  18.4 6.7 %collective-permute-start.5 = (f32[2,64,128]{2,1,0:T(8,128)}, f32[2,64,128]{2,1,0:T(8,128)S(1)}, u32[]{:S(2)}, u32[]{:S(2)}) collective-permute-start(f32[2,64,128]{2,1,0:T(8,128)} %pad.8), channel_id=1, source_target_pairs={{1,0},{2,1},{3,2},{0,3},{5,4},{6,5},{7,6},{4,7},{9,8},{10,9},{11,1... | collective-permute-start | bytes 196616 | tf_op jit(solution)/shard_map/ppermute | solution.py:34
  20.2 4.9 %collective-permute-start.3 = (f32[2,32,128]{2,1,0:T(8,128)}, f32[2,32,128]{2,1,0:T(8,128)}, u32[]{:S(2)}, u32[]{:S(2)}) collective-permute-start(f32[2,32,128]{2,1,0:T(8,128)} %bitcast.32), channel_id=1, source_target_pairs={{4,0},{8,4},{12,8},{0,12},{5,1},{9,5},{13,9},{1,13},{6,2},{10,6},{... | collective-permute-start | bytes 98312 | tf_op jit(solution)/shard_map/ppermute | solution.py:34
  25.1 0.7 copy-start.2

commit v2 on v1

--- a/solution.py
+++ b/solution.py
@@ -152,37 +152,64 @@
     lax.fori_loop(0, nblk // group, place, 0)
 
 
-def exchange_kernel(n_x, n_y, send, recv, send_sem, recv_sem):
+def exchange_kernel(
+    n_x, n_y, n_z, send, squares, recv, total, near, far, send_sem, recv_sem, part_send, part_recv,
+    own_sem,
+):
     a, b = lax.axis_index("gx"), lax.axis_index("gy")
     c = lax.axis_index("wa")
     me = a * n_y + b
     offsets = [(i, j) for i in range(n_x) for j in range(n_y) if i or j]
     offsets.sort(key=lambda o: (bool(o[0]) and bool(o[1]), min(o[1], n_y - o[1])))
+    peers = [(lax.rem(a + i, n_x), lax.rem(b + j, n_y), c) for i, j in offsets]
+    mates = [(a, b, lax.rem(c + k, n_z)) for k in range(1, n_z)]
     barrier = pltpu.get_barrier_semaphore()
-    peers = [(lax.rem(a + i, n_x), lax.rem(b + j, n_y)) for i, j in offsets]
-    for pa, pb in peers:
-        pl.semaphore_signal(barrier, inc=1, device_id=(pa, pb, c), device_id_type=MESH)
-    pl.semaphore_wait(barrier, len(peers))
-    copies = []
-    for k, (pa, pb) in enumerate(peers):
+    for device in mates + peers:
+        pl.semaphore_signal(barrier, inc=1, device_id=device, device_id_type=MESH)
+    pl.semaphore_wait(barrier, len(peers) + len(mates))
+
+    def start(src, dst, sems, device):
         copy = pltpu.make_async_remote_copy(
-            src_ref=send.at[:, pa * n_y + pb],
-            dst_ref=recv.at[:, me],
-            send_sem=send_sem.at[k],
-            recv_sem=recv_sem.at[k],
-            device_id=(pa, pb, c),
+            src_ref=src,
+            dst_ref=dst,
+            send_sem=sems[0],
+            recv_sem=sems[1],
+            device_id=device,
             device_id_type=MESH,
         )
         copy.start()
-        copies.append(copy)
+        return copy
+
+    own = pltpu.make_async_copy(squares, near.at[c], own_sem)
+    own.start()
+    first = [
+        start(squares, near.at[c], (part_send.at[k], part_recv.at[k]), device)
+        for k, device in enumerate(mates)
+    ]
+    copies = [
+        start(
+            send.at[:, device[0] * n_y + device[1]],
+            recv.at[:, me],
+            (send_sem.at[k], recv_sem.at[k]),
+            device,
+        )
+        for k, device in enumerate(peers)
+    ]
+    own.wait()
+    for copy in first:
+        copy.wait()
+    for k, device in enumerate(peers):
+        sem = n_z - 1 + k
+        copies.append(start(near, far.at[k], (part_send.at[sem], part_recv.at[sem]), device))
     for copy in copies:
         copy.wait()
+    total[...] = jnp.sum(near[...], axis=0) + jnp.sum(far[...], axis=(0, 1))
 
 
 def scale_kernel(every, me, squares, recv, send, out):
     total = jnp.sum(squares[...], keepdims=True)
     scale = 1.0 / jnp.sqrt(total / every + 1e-06)
-    own = pl.program_id(1) == me[0]
+    own = pl.program_id(0) == me[0]
 
     @pl.when(own)
     def _():
@@ -235,34 +262,41 @@
     outgoing = outgoing.reshape(comps, writers, capacity, width)
 
     anywhere = pl.BlockSpec(memory_space=pl.ANY)
-    arrived = pl.pallas_call(
-        functools.partial(exchange_kernel, n_x, n_y),
-        out_shape=jax.ShapeDtypeStruct(outgoing.shape, f32),
-        in_specs=[anywhere],
-        out_specs=anywhere,
+    arrived, squares = pl.pallas_call(
+        functools.partial(exchange_kernel, n_x, n_y, n_z),
+        out_shape=(
+            jax.ShapeDtypeStruct(outgoing.shape, f32),
+            jax.ShapeDtypeStruct(squares.shape, f32),
+        ),
+        in_specs=[anywhere, vmem],
+        out_specs=(anywhere, vmem),
         scratch_shapes=[
+            pltpu.VMEM((n_z,) + squares.shape, f32),
+            pltpu.VMEM((writers - 1, n_z) + squares.shape, f32),
             pltpu.SemaphoreType.DMA((writers - 1,)),
             pltpu.SemaphoreType.DMA((writers - 1,)),
+            pltpu.SemaphoreType.DMA((writers + n_z - 2,)),
+            pltpu.SemaphoreType.DMA((writers + n_z - 2,)),
+            pltpu.SemaphoreType.DMA,
         ],
         compiler_params=pltpu.CompilerParams(collective_id=0, has_side_effects=True),
         name="exchange",
-    )(outgoing)
-
-    squares = lax.psum(squares, ("gx", "gy", "wa"))
+    )(outgoing, squares)
+
     every = velocity.size * n_x * n_y * n_z
     me = (lax.axis_index("gx") * n_y + lax.axis_index("gy")).astype(jnp.int32).reshape(1)
-    block = (1, 1, capacity, width)
+    block = (comps, 1, capacity, width)
     received = pl.pallas_call(
         functools.partial(scale_kernel, float(every)),
         grid_spec=pltpu.PrefetchScalarGridSpec(
             num_scalar_prefetch=1,
-            grid=(comps, writers),
+            grid=(writers,),
             in_specs=[
-                pl.BlockSpec((8, cells_z), lambda i, s, me: (0, 0)),
-                pl.BlockSpec(block, lambda i, s, me: (i, s, 0, 0)),
-                pl.BlockSpec(block, lambda i, s, me: (i, me[0], 0, 0)),
+                pl.BlockSpec((8, cells_z), lambda s, me: (0, 0)),
+                pl.BlockSpec(block, lambda s, me: (0, s, 0, 0)),
+                pl.BlockSpec(block, lambda s, me: (0, me[0], 0, 0)),
             ],
-            out_specs=pl.BlockSpec(block, lambda i, s, me: (i, s, 0, 0)),
+            out_specs=pl.BlockSpec(block, lambda s, me: (0, s, 0, 0)),
         ),
         out_shape=jax.ShapeDtypeStruct(outgoing.shape, f32),
         name="scale",

time: 247 us -> 205 us (0.83)
  blocking collectives: 39.7 us -> 0 us
    psum x1 -> x0, blocking collectives: 39.7 us -> none  [local(): squares = lax.psum(squares, ('gx', 'gy', 'wa'))]
    pallas_call x1, Pallas kernels: 16.2 us -> 8.57 us  [local(): pl.pallas_call(functools.partial(scale_kernel, float(every)), grid_spec=p...]
    pallas_call x1, Pallas kernels: 139 us -> 145 us  [local(): pl.pallas_call(functools.partial(exchange_kernel, n_x, n_y, n_z), out_sha...]
    unnamed x10 -> x12, local copies, waits for them, and re-layouts: 5.93 us -> 6.52 us
  transfers between devices with their start and end apart: 6 -> 6, of which waited for: 0 -> 0; matrix products, arithmetic and copies ran while one was open for 5% -> 6% of each run, Pallas kernels for 1% -> 1%
where the time goes in v2:
time: 205 us
  Pallas kernels  181 us (88%)
  local copies, waits for them, and re-layouts  14.6 us (7%)
  starting transfers between devices  8.85 us (4%)
    pallas_call x1, Pallas kernels, local(): pl.pallas_call(functools.partial(exchange_kernel, n_x, n_y, n_z), out_sha...  145 us
    pallas_call x1, Pallas kernels, local(): pl.pallas_call(blocks_kernel, out_shape=(jax.ShapeDtypeStruct((comps * wr...  24.9 us
    ppermute x6, starting transfers between devices, faces(): return (lax.ppermute(last, axis, up), lax.ppermute(first, axis, down))  8.85 us
    pallas_call x1, Pallas kernels, local(): pl.pallas_call(functools.partial(scale_kernel, float(every)), grid_spec=p...  8.57 us
    unnamed x12, local copies, waits for them, and re-layouts  6.52 us
  transfers between devices with their start and end apart: 6, of which 0 were waited for; matrix products, arithmetic and copies ran while one was open for 6% of the time, Pallas kernels for 1%

profile of v2, /device:TPU:0, one launch (start us, length us, event | category | flops | bytes accessed | tf_op | source)
XLA Modules:
  0.0 204.8 jit_solution(13779645267904347390)
XLA Ops:
  0.0 1.7 slice_bitcast_fusion
  1.7 3.0 %collective-permute-start.1 = (f32[2,64,128]{2,1,0:T(8,128)}, f32[2,64,128]{2,1,0:T(8,128)S(1)}, u32[]{:S(2)}, u32[]{:S(2)}) collective-permute-start(f32[2,64,128]{2,1,0:T(8,128)} %get-tuple-element.15), channel_id=1, source_target_pairs={{16,0},{0,16},{17,1},{1,17},{18,2},{2,18},{19,3},{3,19},{20,4},{4,... | collective-permute-start | bytes 196616 | tf_op jit(solution)/shard_map/ppermute | solution.py:34
  4.6 0.0 collective-permute-start
  4.7 1.7 slice.29
  6.4 0.7 fusion.1
  7.1 2.1 %collective-permute-start.2 = (f32[2,32,128]{2,1,0:T(8,128)}, f32[2,32,128]{2,1,0:T(8,128)}, u32[]{:S(2)}, u32[]{:S(2)}) collective-permute-start(f32[2,32,128]{2,1,0:T(8,128)} %bitcast.6), channel_id=1, source_target_pairs={{0,4},{4,8},{8,12},{12,0},{1,5},{5,9},{9,13},{13,1},{2,6},{6,10},{... | collective-permute-start | bytes 98312 | tf_op jit(solution)/shard_map/ppermute | solution.py:34
  9.1 2.8 %fusion = (f32[2,32,64,1]{3,2,1,0:T(8,128)}, f32[2,32,64,1]{3,2,1,0:T(8,128)}) fusion(f32[3,32,64,128]{3,2,1,0:T(8,128)S(1)} %copy-done), kind=kLoop, calls=%fused_computation.2 | loop fusion | bytes 65536 | tf_op jit(solution)/shard_map/slice | solution.py:239
  11.9 2.6 %copy.15 = f32[2,32,64,1]{1,2,0,3:T(8,128)S(1)} copy(f32[2,32,64,1]{3,2,1,0:T(8,128)} %get-tuple-element.14) | data formatting | bytes 32768
  14.6 0.6 pad.7
  15.2 0.0 collective-permute-start.4
  15.2 2.6 %copy.16 = f32[2,32,64,1]{1,2,0,3:T(8,128)S(1)} copy(f32[2,32,64,1]{3,2,1,0:T(8,128)} %get-tuple-element.13) | data formatting | bytes 32768
  17.8 0.6 pad.8
  18.4 1.7 collective-permute-start.5
  20.2 0.0 collective-permute-done.2.yb
  20.2 2.0 collective-permute-start.3
  22.2 2.9 %slots.1 = s32[16,128]{1,0:T(8,128)} custom-call(s32[16,128]{1,0:T(8,128)} %bitcast.33), custom_call_target="tpu_custom_call" | custom-call | tf_op jit(solution)/shard_map/slots/pallas_call | solution.py:241
  25.1 0.0 collective-permute-done.3.ya
  25.1 0.0 collective-permute-done.1.xa
  25.1 0.0 collective-permute-done.xb
  25.1 0.7 copy-done.2
  25.8 24.9 %blocks.1 = (f32[12288,128]{1,0:T(8,128)}, f32[8,128]{1,0:T(8,128)S(1)}) custom-call(s32[2048]{0:T(1024)S(1)} %bitcast.26, s32[2048]{0:T(1024)S(1)} %bitcast.27, f32[3,32,64,128]{3,2,1,0:T(8,128)S(1)} %copy-done, f32[2,64,128]{2,1,0:T(8,128)S(1)} %collective-permute-done.xb, f32[2,64,128]{2,1,0:T(8,128)S(1)} %collective-permute-done.1.xa, ...), custom_call_target="tpu_custom_call" | custom-call | tf_op jit(solution)/shard_map/blocks/pallas_call | solution.py:250
  50.7 0.6 copy-done.4
  51.3 144.9 %exchange.1 = (f32[3,8,512,128]{3,2,1,0:T(8,128)}, f32[8,128]{1,0:T(8,128)}) custom-call(f32[3,8,512,128]{3,2,1,0:T(8,128)} %bitcast.28, f32[8,128]{1,0:T(8,128)} %copy-done.4), custom_call_target="tpu_custom_call" | custom-call | tf_op jit(solution)/shard_map/exchange/pallas_call | solution.py:265
  196.2 8.6 %scale.1 = f32[3,8,512,128]{3,2,1,0:T(8,128)} custom-call(s32[1]{0:T(128)} %bitcast.me, f32[8,128]{1,0:T(8,128)} %get-tuple-element.11.squares, f32[3,8,512,128]{3,2,1,0:T(8,128)} %get-tuple-element.12.recv, f32[3,8,512,128]{3,2,1,0:T(8,128)} %bitcast.29), custom_call_target="tpu_custom_call" | custom-call | tf_op jit(solution)/shard_map/scale/pallas_call | solution.py:289
  (10 shorter events, 0.0 us)
Async XLA Ops:
  0.0 9.1 %copy-start = (f32[3,32,64,128]{3,2,1,0:T(8,128)S(1)}, f32[3,32,64,128]{3,2,1,0:T(8,128)}, u32[]{:S(2)}) copy-start(f32[3,32,64,128]{3,2,1,0:T(8,128)} %vel.1) | copy-start | bytes 9437188
  1.7 23.4 %collective-permute-start.1 = (f32[2,64,128]{2,1,0:T(8,128)}, f32[2,64,128]{2,1,0:T(8,128)S(1)}, u32[]{:S(2)}, u32[]{:S(2)}) collective-permute-start(f32[2,64,128]{2,1,0:T(8,128)} %get-tuple-element.15), channel_id=1, source_target_pairs={{16,0},{0,16},{17,1},{1,17},{18,2},{2,18},{19,3},{3,19},{20,4},{4,... | collective-permute-start | bytes 196616 | tf_op jit(solution)/shard_map/ppermute | solution.py:34
  4.6 20.4 %collective-permute-start = (f32[2,64,128]{2,1,0:T(8,128)}, f32[2,64,128]{2,1,0:T(8,128)S(1)}, u32[]{:S(2)}, u32[]{:S(2)}) collective-permute-start(f32[2,64,128]{2,1,0:T(8,128)} %get-tuple-element.16), channel_id=1, source_target_pairs={{0,16},{16,0},{1,17},{17,1},{2,18},{18,2},{3,19},{19,3},{4,20},{20... | collective-permute-start | bytes 196616 | tf_op jit(solution)/shard_map/ppermute | solution.py:34
  7.1 13.1 %collective-permute-start.2 = (f32[2,32,128]{2,1,0:T(8,128)}, f32[2,32,128]{2,1,0:T(8,128)}, u32[]{:S(2)}, u32[]{:S(2)}) collective-permute-start(f32[2,32,128]{2,1,0:T(8,128)} %bitcast.6), channel_id=1, source_target_pairs={{0,4},{4,8},{8,12},{12,0},{1,5},{5,9},{9,13},{13,1},{2,6},{6,10},{... | collective-permute-start | bytes 98312 | tf_op jit(solution)/shard_map/ppermute | solution.py:34
  11.9 13.2 %copy-start.1 = (bf16[256,256]{1,0:T(8,128)(2,1)S(1)}, bf16[256,256]{1,0:T(8,128)(2,1)}, u32[]{:S(2)}) copy-start(bf16[256,256]{1,0:T(8,128)(2,1)} %constant.18.clone.table) | copy-start | bytes 393220
  11.9 13.2 %copy-start.3 = (s32[1,1,1,2048]{3,2,1,0:T(1,128)S(1)}, s32[1,1,1,2048]{3,2,1,0:T(1,128)}, u32[]{:S(2)}) copy-start(s32[1,1,1,2048]{3,2,1,0:T(1,128)} %param.5) | copy-start | bytes 24580
  15.2 9.9 %collective-permute-start.4 = (f32[2,64,128]{2,1,0:T(8,128)}, f32[2,64,128]{2,1,0:T(8,128)S(1)}, u32[]{:S(2)}, u32[]{:S(2)}) collective-permute-start(f32[2,64,128]{2,1,0:T(8,128)} %pad.7), channel_id=1, source_target_pairs={{0,1},{1,2},{2,3},{3,0},{4,5},{5,6},{6,7},{7,4},{8,9},{9,10},{10,1... | collective-permute-start | bytes 196616 | tf_op jit(solution)/shard_map/ppermute | solution.py:34
  18.4 6.7 %collective-permute-start.5 = (f32[2,64,128]{2,1,0:T(8,128)}, f32[2,64,128]{2,1,0:T(8,128)S(1)}, u32[]{:S(2)}, u32[]{:S(2)}) collective-permute-start(f32[2,64,128]{2,1,0:T(8,128)} %pad.8), channel_id=1, source_target_pairs={{1,0},{2,1},{3,2},{0,3},{5,4},{6,5},{7,6},{4,7},{9,8},{10,9},{11,1... | collective-permute-start | bytes 196616 | tf_op jit(solution)/shard_map/ppermute | solution.py:34
  20.2 4.9 %collective-permute-start.3 = (f32[2,32,128]{2,1,0:T(8,128)}, f32[2,32,128]{2,1,0:T(8,128)}, u32[]{:S(2)}, u32[]{:S(2)}) collective-permute-start(f32[2,32,128]{2,1,0:T(8,128)} %bitcast.32), channel_id=1, source_target_pairs={{4,0},{8,4},{12,8},{0,12},{5,1},{9,5},{13,9},{1,13},{6,2},{10,6},{... | collective-permute-start | bytes 98312 | tf_op jit(solution)/shard_map/ppermute | solution.py:34
  25.1 0.7 copy-start.2
  50.7 0.6 copy-start.4

commit v3 on v2

--- a/solution.py
+++ b/solution.py
@@ -26,15 +26,28 @@
     return np.block([[high, low], [high, np.zeros_like(low)]]).astype(jnp.bfloat16)
 
 
-def faces(array, axis):
-    peers = lax.axis_size(axis)
-    up = [(i, (i + 1) % peers) for i in range(peers)]
-    down = [(j, i) for i, j in up]
-    first, last = array
-    return lax.ppermute(last, axis, up), lax.ppermute(first, axis, down)
-
-
-def slot_kernel(writers, capacity, targets, slots):
+def faces_kernel(writers, capacity, targets, vel, slots, y_faces, z_faces):
+    comps, cells_x, cells_y, cells_z = vel.shape
+    lane = lax.broadcasted_iota(jnp.int32, (cells_y, cells_z), 1)
+
+    def plane(x, acc):
+        here = lane == x
+        rolled = [
+            pltpu.roll(vel[comp, x], lax.rem(x + last, cells_z), 1)
+            for last in range(2)
+            for comp in (0, 1)
+        ]
+        for i, comp in enumerate((0, 2)):
+            y_faces[0, i, pl.ds(x, 1), :] = vel[comp, x, 0:1]
+            y_faces[1, i, pl.ds(x, 1), :] = vel[comp, x, cells_y - 1 : cells_y]
+        return tuple(jnp.where(here, new, old) for new, old in zip(rolled, acc))
+
+    zero = jnp.zeros((cells_y, cells_z), jnp.float32)
+    columns = lax.fori_loop(0, cells_x, plane, (zero,) * 4)
+    for last in range(2):
+        for i in range(2):
+            z_faces[last, i] = columns[2 * last + i]
+
     t = targets[...]
     rows, lanes = t.shape
     shape = (lanes, lanes)
@@ -55,6 +68,43 @@
         return jnp.where(mine, w * capacity + rank.astype(jnp.int32), acc)
 
     slots[...] = lax.fori_loop(0, writers, body, jnp.zeros_like(t))
+
+
+def halo_kernel(sizes, vel, y_faces, z_faces, xb, xa, yb, ya, zb, za, send_sem, recv_sem):
+    place = [lax.axis_index(axis) for axis in ("gx", "gy", "wa")]
+    cells_x = vel.shape[1]
+
+    def beside(axis, step):
+        size = sizes[axis]
+        moved = lax.rem(place[axis] + step + size, size)
+        return tuple(moved if i == axis else p for i, p in enumerate(place))
+
+    moves = [
+        (vel.at[pl.ds(1, 2), cells_x - 1], xb, beside(0, 1)),
+        (vel.at[pl.ds(1, 2), 0], xa, beside(0, -1)),
+        (y_faces.at[1], yb, beside(1, 1)),
+        (y_faces.at[0], ya, beside(1, -1)),
+        (z_faces.at[1], zb, beside(2, 1)),
+        (z_faces.at[0], za, beside(2, -1)),
+    ]
+    barrier = pltpu.get_barrier_semaphore()
+    for _, _, device in moves:
+        pl.semaphore_signal(barrier, inc=1, device_id=device, device_id_type=MESH)
+    pl.semaphore_wait(barrier, len(moves))
+    copies = []
+    for k, (src, dst, device) in enumerate(moves):
+        copy = pltpu.make_async_remote_copy(
+            src_ref=src,
+            dst_ref=dst,
+            send_sem=send_sem.at[k],
+            recv_sem=recv_sem.at[k],
+            device_id=device,
+            device_id_type=MESH,
+        )
+        copy.start()
+        copies.append(copy)
+    for copy in copies:
+        copy.wait()
 
 
 def block_rows(plane):
@@ -140,13 +190,15 @@
     group = 8
 
     def place(j, _):
+        found = []
         for k in range(group):
             i = j * group + k
-            slot, keep = slots[i], freqs < lens[i]
+            keep = freqs < lens[i]
             for c in range(comps):
-                out[pl.ds(c * rows + slot, 1), :] = jnp.where(
-                    keep, coeffs[c, pl.ds(i, 1), :], 0.0
-                )
+                cut = jnp.where(keep, coeffs[c, pl.ds(i, 1), :], 0.0)
+                found.append((c * rows + slots[i], cut))
+        for spot, cut in found:
+            out[pl.ds(spot, 1), :] = cut
         return 0
 
     lax.fori_loop(0, nblk // group, place, 0)
@@ -229,24 +281,31 @@
     capacity = max(2, 2 * nblk // writers)
     f32 = jnp.float32
 
-    vw, uw, uv = velocity[1:], velocity[::2], velocity[:2]
-    xb, xa = faces((vw[:, 0], vw[:, -1]), "gx")
-    yb, ya = faces((uw[:, :, 0], uw[:, :, -1]), "gy")
-
-    def z_face(f):
-        return jnp.pad(f.transpose(0, 2, 1), ((0, 0), (0, 0), (0, cells_z - cells_x)))
-
-    zb, za = faces((z_face(uv[..., 0]), z_face(uv[..., -1])), "wa")
-
-    slots = pl.pallas_call(
-        functools.partial(slot_kernel, writers, capacity),
-        out_shape=jax.ShapeDtypeStruct((nblk // 128, 128), jnp.int32),
-        name="slots",
-    )(destinations.reshape(nblk // 128, 128))
-
-    table = jnp.asarray(split_table())
     smem = pl.BlockSpec(memory_space=pltpu.SMEM)
     vmem = pl.BlockSpec(memory_space=pltpu.VMEM)
+    anywhere = pl.BlockSpec(memory_space=pl.ANY)
+    x_face = jax.ShapeDtypeStruct((2, cells_y, cells_z), f32)
+    y_face = jax.ShapeDtypeStruct((2, cells_x, cells_z), f32)
+    slots, y_faces, z_faces = pl.pallas_call(
+        functools.partial(faces_kernel, writers, capacity),
+        out_shape=(
+            jax.ShapeDtypeStruct((nblk // 128, 128), jnp.int32),
+            jax.ShapeDtypeStruct((2,) + y_face.shape, f32),
+            jax.ShapeDtypeStruct((2,) + x_face.shape, f32),
+        ),
+        name="faces",
+    )(destinations.reshape(nblk // 128, 128), velocity)
+    halos = pl.pallas_call(
+        functools.partial(halo_kernel, (n_x, n_y, n_z)),
+        out_shape=(x_face, x_face, y_face, y_face, x_face, x_face),
+        in_specs=[anywhere] * 3,
+        out_specs=(anywhere,) * 6,
+        scratch_shapes=[pltpu.SemaphoreType.DMA((6,)), pltpu.SemaphoreType.DMA((6,))],
+        compiler_params=pltpu.CompilerParams(collective_id=1, has_side_effects=True),
+        name="halo",
+    )(velocity, y_faces, z_faces)
+
+    table = jnp.asarray(split_table())
     outgoing, squares = pl.pallas_call(
         blocks_kernel,
         out_shape=(
@@ -258,10 +317,9 @@
         scratch_shapes=[pltpu.VMEM((comps, nblk, width), f32)],
         compiler_params=pltpu.CompilerParams(vmem_limit_bytes=48 * 2**20),
         name="blocks",
-    )(slots.reshape(nblk), lengths.reshape(nblk), velocity, xb, xa, yb, ya, zb, za, table)
+    )(slots.reshape(nblk), lengths.reshape(nblk), velocity, *halos, table)
     outgoing = outgoing.reshape(comps, writers, capacity, width)
 
-    anywhere = pl.BlockSpec(memory_space=pl.ANY)
     arrived, squares = pl.pallas_call(
         functools.partial(exchange_kernel, n_x, n_y, n_z),
         out_shape=(

time: 205 us -> 202 us (0.985)
  Pallas kernels: 181 us -> 195 us
  starting transfers between devices: 8.85 us -> 0 us
  local copies, waits for them, and re-layouts: 14.6 us -> 6.16 us
    pallas_call x1 -> x2, Pallas kernels: 2.88 us -> 17.8 us  [the longest x1 10.2 us: local(): pl.pallas_call(functools.partial(halo_kernel, (n_x, n_y, n_z)), out_shape...]
    ppermute x6 -> x0, starting transfers between devices: 8.85 us -> none  [faces(): return (lax.ppermute(last, axis, up), lax.ppermute(first, axis, down))]
    slice x3 -> x0, local copies, waits for them, and re-layouts: 5.16 us -> none  [the longest x1 2.77 us: local(): zb, za = faces((z_face(uv[..., 0]), z_face(uv[..., -1])), 'wa')]
    unnamed x12 -> x22, local copies, waits for them, and re-layouts: 6.52 us -> 6.16 us
  transfers between devices with their start and end apart: 6 -> 0, of which waited for: 0 -> 0; matrix products, arithmetic and copies ran while one was open for 6% -> 0% of each run, Pallas kernels for 1% -> 0%
where the time goes in v3:
time: 202 us; the launch traced here: 201 us
  Pallas kernels  195 us (97%)
  local copies, waits for them, and re-layouts  6.16 us (3%)
    pallas_call x1, Pallas kernels, local(): pl.pallas_call(functools.partial(exchange_kernel, n_x, n_y, n_z), out_sha...  144 us
    pallas_call x1, Pallas kernels, local(): pl.pallas_call(blocks_kernel, out_shape=(jax.ShapeDtypeStruct((comps * wr...  25 us
    pallas_call x1, Pallas kernels, local(): pl.pallas_call(functools.partial(halo_kernel, (n_x, n_y, n_z)), out_shape...  10.2 us
    pallas_call x1, Pallas kernels, local(): pl.pallas_call(functools.partial(scale_kernel, float(every)), grid_spec=p...  8.57 us
    pallas_call x1, Pallas kernels, local(): pl.pallas_call(functools.partial(faces_kernel, writers, capacity), out_sh...  7.57 us
    unnamed x22, local copies, waits for them, and re-layouts  6.16 us

profile of v3, /device:TPU:0, one launch (start us, length us, event | category | flops | bytes accessed | tf_op | source)
XLA Modules:
  0.0 201.3 jit_solution(5253070227557919380)
XLA Ops:
  0.0 0.0 copy-start
  0.0 0.0 copy-start.8
  0.0 7.6 %faces.1 = (s32[16,128]{1,0:T(8,128)}, f32[2,2,32,128]{3,2,1,0:T(8,128)}, f32[2,2,64,128]{3,2,1,0:T(8,128)}) custom-call(s32[16,128]{1,0:T(8,128)} %bitcast.10, f32[3,32,64,128]{3,2,1,0:T(8,128)} %vel.5), custom_call_target="tpu_custom_call" | custom-call | tf_op jit(solution)/shard_map/faces/pallas_call | solution.py:289
  7.6 10.2 %halo.1 = (f32[2,64,128]{2,1,0:T(8,128)}, f32[2,64,128]{2,1,0:T(8,128)}, f32[2,32,128]{2,1,0:T(8,128)}, f32[2,32,128]{2,1,0:T(8,128)}, f32[2,64,128]{2,1,0:T(8,128)}, /*index=5*/f32[2,64,128]{2,1,0:T(8,128)}) custom-call(f32[3,32,64,128]{3,2,1,0:T(8,128)} %vel.5, f32[2,2,32,128]{3,2,1,0:T(8,128)} %get-tuple-element.19.y_faces, ...), custom_call_target="tpu_custom_call" | custom-call | tf_op jit(solution)/shard_map/halo/pallas_call | solution.py:298
  17.8 0.0 copy-done.1
  17.8 0.0 copy-done
  17.8 0.0 copy-done.8
  17.8 0.0 copy-start.2
  17.9 0.8 copy-done.2
  18.7 0.0 copy-start.3
  18.7 0.8 copy-done.3
  19.5 0.0 copy-start.4
  19.5 0.8 copy-done.4
  20.4 0.0 copy-start.5
  20.4 0.8 copy-done.5
  21.2 0.0 copy-start.6
  21.2 0.8 copy-done.6
  22.0 0.0 copy-start.7
  22.0 0.8 copy-done.7
  22.7 0.7 copy-done.9
  23.4 25.0 %blocks.1 = (f32[12288,128]{1,0:T(8,128)}, f32[8,128]{1,0:T(8,128)S(1)}) custom-call(s32[2048]{0:T(1024)S(1)} %bitcast.7, s32[2048]{0:T(1024)S(1)} %bitcast.6, f32[3,32,64,128]{3,2,1,0:T(8,128)S(1)} %copy-done, f32[2,64,128]{2,1,0:T(8,128)S(1)} %copy-done.2, f32[2,64,128]{2,1,0:T(8,128)S(1)} %copy-done.3, f32[2,32,128]{2,1,0:T(8,128)S(1)} %copy-done.6, ...), custom_call_target="tpu_custom_call" | custom-call | tf_op jit(solution)/shard_map/blocks/pallas_call | solution.py:309
  48.4 0.6 copy-done.10
  49.0 143.7 %exchange.1 = (f32[3,8,512,128]{3,2,1,0:T(8,128)}, f32[8,128]{1,0:T(8,128)}) custom-call(f32[3,8,512,128]{3,2,1,0:T(8,128)} %bitcast.8, f32[8,128]{1,0:T(8,128)} %copy-done.10), custom_call_target="tpu_custom_call" | custom-call | tf_op jit(solution)/shard_map/exchange/pallas_call | solution.py:323
  192.7 8.6 %scale.1 = f32[3,8,512,128]{3,2,1,0:T(8,128)} custom-call(s32[1]{0:T(128)} %bitcast.me, f32[8,128]{1,0:T(8,128)} %get-tuple-element.29.squares, f32[3,8,512,128]{3,2,1,0:T(8,128)} %get-tuple-element.30.recv, f32[3,8,512,128]{3,2,1,0:T(8,128)} %bitcast.9), custom_call_target="tpu_custom_call" | custom-call | tf_op jit(solution)/shard_map/scale/pallas_call | solution.py:347
  (3 shorter events, 0.0 us)
Async XLA Ops:
  0.0 17.8 %copy-start.1 = (bf16[256,256]{1,0:T(8,128)(2,1)S(1)}, bf16[256,256]{1,0:T(8,128)(2,1)}, u32[]{:S(2)}) copy-start(bf16[256,256]{1,0:T(8,128)(2,1)} %constant.15.clone.table) | copy-start | bytes 393220
  0.0 17.8 %copy-start = (f32[3,32,64,128]{3,2,1,0:T(8,128)S(1)}, f32[3,32,64,128]{3,2,1,0:T(8,128)}, u32[]{:S(2)}) copy-start(f32[3,32,64,128]{3,2,1,0:T(8,128)} %vel.5) | copy-start | bytes 9437188
  0.0 17.8 %copy-start.8 = (s32[1,1,1,2048]{3,2,1,0:T(1,128)S(1)}, s32[1,1,1,2048]{3,2,1,0:T(1,128)}, u32[]{:S(2)}) copy-start(s32[1,1,1,2048]{3,2,1,0:T(1,128)} %param.5) | copy-start | bytes 24580
  17.8 0.8 copy-start.2
  18.7 0.8 copy-start.3
  19.5 0.8 copy-start.4
  20.4 0.8 copy-start.5
  21.2 0.8 copy-start.6
  22.0 0.8 copy-start.7
  22.7 0.7 copy-start.9
  48.4 0.6 copy-start.10

commit v4 on v3

--- a/solution.py
+++ b/solution.py
@@ -70,7 +70,7 @@
     slots[...] = lax.fori_loop(0, writers, body, jnp.zeros_like(t))
 
 
-def halo_kernel(sizes, vel, y_faces, z_faces, xb, xa, yb, ya, zb, za, send_sem, recv_sem):
+def halo_kernel(sizes, vel, y_faces, z_faces, halos, send_sem, recv_sem):
     place = [lax.axis_index(axis) for axis in ("gx", "gy", "wa")]
     cells_x = vel.shape[1]
 
@@ -79,13 +79,14 @@
         moved = lax.rem(place[axis] + step + size, size)
         return tuple(moved if i == axis else p for i, p in enumerate(place))
 
+    across, along = pl.ds(0, vel.shape[2]), pl.ds(0, cells_x)
     moves = [
-        (vel.at[pl.ds(1, 2), cells_x - 1], xb, beside(0, 1)),
-        (vel.at[pl.ds(1, 2), 0], xa, beside(0, -1)),
-        (y_faces.at[1], yb, beside(1, 1)),
-        (y_faces.at[0], ya, beside(1, -1)),
-        (z_faces.at[1], zb, beside(2, 1)),
-        (z_faces.at[0], za, beside(2, -1)),
+        (vel.at[pl.ds(1, 2), cells_x - 1], halos.at[0, :, across], beside(0, 1)),
+        (vel.at[pl.ds(1, 2), 0], halos.at[1, :, across], beside(0, -1)),
+        (y_faces.at[1], halos.at[2, :, along], beside(1, 1)),
+        (y_faces.at[0], halos.at[3, :, along], beside(1, -1)),
+        (z_faces.at[1], halos.at[4, :, across], beside(2, 1)),
+        (z_faces.at[0], halos.at[5, :, across], beside(2, -1)),
     ]
     barrier = pltpu.get_barrier_semaphore()
     for _, _, device in moves:
@@ -122,9 +123,7 @@
     return tiles.reshape(cells_y, cells_z)
 
 
-def blocks_kernel(
-    slots, lens, vel, xb, xa, yb, ya, zb, za, table, out, squares, coeffs
-):
+def blocks_kernel(slots, lens, vel, halos, table, out, squares, coeffs):
     comps, cells_x, cells_y, cells_z = vel.shape
     nblk = coeffs.shape[1]
     per_plane = nblk // cells_x
@@ -147,21 +146,21 @@
 
         def along_x(comp):
             nxt = jnp.where(
-                x == cells_x - 1, xa[comp - 1], vel[comp, jnp.minimum(x + 1, cells_x - 1)]
+                x == cells_x - 1, halos[1, comp - 1, :cells_y], vel[comp, jnp.minimum(x + 1, cells_x - 1)]
             )
-            prv = jnp.where(x == 0, xb[comp - 1], vel[comp, jnp.maximum(x - 1, 0)])
+            prv = jnp.where(x == 0, halos[0, comp - 1, :cells_y], vel[comp, jnp.maximum(x - 1, 0)])
             return (nxt - prv) * 0.5
 
         def along_y(f, face):
             nxt = jnp.where(
-                row == cells_y - 1, ya[face, pl.ds(x, 1), :], pltpu.roll(f, cells_y - 1, 0)
+                row == cells_y - 1, halos[3, face, pl.ds(x, 1), :], pltpu.roll(f, cells_y - 1, 0)
             )
-            prv = jnp.where(row == 0, yb[face, pl.ds(x, 1), :], pltpu.roll(f, 1, 0))
+            prv = jnp.where(row == 0, halos[2, face, pl.ds(x, 1), :], pltpu.roll(f, 1, 0))
             return (nxt - prv) * 0.5
 
         def along_z(f, face):
-            after = pltpu.roll(za[face], cells_z - 1 - x, 1)
-            before = pltpu.roll(zb[face], lax.rem(cells_z - x, cells_z), 1)
+            after = pltpu.roll(halos[5, face, :cells_y], cells_z - 1 - x, 1)
+            before = pltpu.roll(halos[4, face, :cells_y], lax.rem(cells_z - x, cells_z), 1)
             nxt = jnp.where(lane == cells_z - 1, after, pltpu.roll(f, cells_z - 1, 1))
             prv = jnp.where(lane == 0, before, pltpu.roll(f, 1, 1))
             return (nxt - prv) * 0.5
@@ -185,23 +184,28 @@
             coeffs[c, pl.ds(start, per_plane), :] = result[c * per_plane : (c + 1) * per_plane]
         return acc
 
-    squares[...] = lax.fori_loop(0, cells_x, plane, jnp.zeros((8, cells_z), jnp.float32))
     freqs = lax.broadcasted_iota(jnp.int32, (1, width), 1)
     group = 8
 
-    def place(j, _):
-        found = []
-        for k in range(group):
-            i = j * group + k
-            keep = freqs < lens[i]
-            for c in range(comps):
-                cut = jnp.where(keep, coeffs[c, pl.ds(i, 1), :], 0.0)
-                found.append((c * rows + slots[i], cut))
-        for spot, cut in found:
-            out[pl.ds(spot, 1), :] = cut
-        return 0
-
-    lax.fori_loop(0, nblk // group, place, 0)
+    def place(x):
+        for start in range(0, per_plane, group):
+            found = []
+            for k in range(start, min(start + group, per_plane)):
+                i = x * per_plane + k
+                keep = freqs < lens[i]
+                for c in range(comps):
+                    cut = jnp.where(keep, coeffs[c, pl.ds(i, 1), :], 0.0)
+                    found.append((c * rows + slots[i], cut))
+            for spot, cut in found:
+                out[pl.ds(spot, 1), :] = cut
+
+    def step(x, acc):
+        place(x - 1)
+        return plane(x, acc)
+
+    first = plane(0, jnp.zeros((8, cells_z), jnp.float32))
+    squares[...] = lax.fori_loop(1, cells_x, step, first)
+    place(cells_x - 1)
 
 
 def exchange_kernel(
@@ -238,21 +242,24 @@
         start(squares, near.at[c], (part_send.at[k], part_recv.at[k]), device)
         for k, device in enumerate(mates)
     ]
-    copies = [
-        start(
+    def blocks_to(k):
+        device = peers[k]
+        return start(
             send.at[:, device[0] * n_y + device[1]],
             recv.at[:, me],
             (send_sem.at[k], recv_sem.at[k]),
             device,
         )
-        for k, device in enumerate(peers)
-    ]
+
+    ahead = min(3, len(peers))
+    copies = [blocks_to(k) for k in range(ahead)]
     own.wait()
     for copy in first:
         copy.wait()
     for k, device in enumerate(peers):
         sem = n_z - 1 + k
         copies.append(start(near, far.at[k], (part_send.at[sem], part_recv.at[sem]), device))
+    copies += [blocks_to(k) for k in range(ahead, len(peers))]
     for copy in copies:
         copy.wait()
     total[...] = jnp.sum(near[...], axis=0) + jnp.sum(far[...], axis=(0, 1))
@@ -284,22 +291,20 @@
     smem = pl.BlockSpec(memory_space=pltpu.SMEM)
     vmem = pl.BlockSpec(memory_space=pltpu.VMEM)
     anywhere = pl.BlockSpec(memory_space=pl.ANY)
-    x_face = jax.ShapeDtypeStruct((2, cells_y, cells_z), f32)
-    y_face = jax.ShapeDtypeStruct((2, cells_x, cells_z), f32)
     slots, y_faces, z_faces = pl.pallas_call(
         functools.partial(faces_kernel, writers, capacity),
         out_shape=(
             jax.ShapeDtypeStruct((nblk // 128, 128), jnp.int32),
-            jax.ShapeDtypeStruct((2,) + y_face.shape, f32),
-            jax.ShapeDtypeStruct((2,) + x_face.shape, f32),
+            jax.ShapeDtypeStruct((2, 2, cells_x, cells_z), f32),
+            jax.ShapeDtypeStruct((2, 2, cells_y, cells_z), f32),
         ),
         name="faces",
     )(destinations.reshape(nblk // 128, 128), velocity)
     halos = pl.pallas_call(
         functools.partial(halo_kernel, (n_x, n_y, n_z)),
-        out_shape=(x_face, x_face, y_face, y_face, x_face, x_face),
+        out_shape=jax.ShapeDtypeStruct((6, 2, max(cells_x, cells_y), cells_z), f32),
         in_specs=[anywhere] * 3,
-        out_specs=(anywhere,) * 6,
+        out_specs=anywhere,
         scratch_shapes=[pltpu.SemaphoreType.DMA((6,)), pltpu.SemaphoreType.DMA((6,))],
         compiler_params=pltpu.CompilerParams(collective_id=1, has_side_effects=True),
         name="halo",
@@ -312,12 +317,12 @@
             jax.ShapeDtypeStruct((comps * writers * capacity, width), f32),
             jax.ShapeDtypeStruct((8, cells_z), f32),
         ),
-        in_specs=[smem, smem] + [vmem] * 8,
+        in_specs=[smem, smem] + [vmem] * 3,
         out_specs=(vmem, vmem),
         scratch_shapes=[pltpu.VMEM((comps, nblk, width), f32)],
         compiler_params=pltpu.CompilerParams(vmem_limit_bytes=48 * 2**20),
         name="blocks",
-    )(slots.reshape(nblk), lengths.reshape(nblk), velocity, *halos, table)
+    )(slots.reshape(nblk), lengths.reshape(nblk), velocity, halos, table)
     outgoing = outgoing.reshape(comps, writers, capacity, width)
 
     arrived, squares = pl.pallas_call(

time: 202 us -> 194 us (0.960)
  Pallas kernels: 195 us -> 191 us
  local copies, waits for them, and re-layouts: 6.16 us -> 2.29 us
    unnamed x22 -> x12, local copies, waits for them, and re-layouts: 6.16 us -> 2.29 us
    pallas_call x1, Pallas kernels: 25 us -> 21.3 us  [local(): pl.pallas_call(blocks_kernel, out_shape=(jax.ShapeDtypeStruct((comps * wr...]
where the time goes in v4:
time: 194 us
  Pallas kernels  191 us (98%)
  local copies, waits for them, and re-layouts  2.29 us (1%)
    pallas_call x1, Pallas kernels, local(): pl.pallas_call(functools.partial(exchange_kernel, n_x, n_y, n_z), out_sha...  144 us
    pallas_call x1, Pallas kernels, local(): pl.pallas_call(blocks_kernel, out_shape=(jax.ShapeDtypeStruct((comps * wr...  21.3 us
    pallas_call x1, Pallas kernels, local(): pl.pallas_call(functools.partial(halo_kernel, (n_x, n_y, n_z)), out_shape...  10.2 us
    pallas_call x1, Pallas kernels, local(): pl.pallas_call(functools.partial(scale_kernel, float(every)), grid_spec=p...  8.57 us
    pallas_call x1, Pallas kernels, local(): pl.pallas_call(functools.partial(faces_kernel, writers, capacity), out_sh...  7.57 us

profile of v4, /device:TPU:0, one launch (start us, length us, event | category | flops | bytes accessed | tf_op | source)
XLA Modules:
  0.0 193.8 jit_solution(12416107457399424088)
XLA Ops:
  0.0 0.0 copy-start.2
  0.0 0.0 copy-start
  0.0 0.0 copy-start.3
  0.0 7.6 %faces.1 = (s32[16,128]{1,0:T(8,128)}, f32[2,2,32,128]{3,2,1,0:T(8,128)}, f32[2,2,64,128]{3,2,1,0:T(8,128)}) custom-call(s32[16,128]{1,0:T(8,128)} %bitcast.10, f32[3,32,64,128]{3,2,1,0:T(8,128)} %vel.5), custom_call_target="tpu_custom_call" | custom-call | tf_op jit(solution)/shard_map/faces/pallas_call | solution.py:294
  7.6 10.2 %halo.1.halos = f32[6,2,64,128]{3,2,1,0:T(8,128)} custom-call(f32[3,32,64,128]{3,2,1,0:T(8,128)} %vel.5, f32[2,2,32,128]{3,2,1,0:T(8,128)} %get-tuple-element.13.y_faces, f32[2,2,64,128]{3,2,1,0:T(8,128)} %get-tuple-element.14.z_faces), custom_call_target="tpu_custom_call" | custom-call | tf_op jit(solution)/shard_map/halo/pallas_call | solution.py:303
  17.8 0.0 copy-done.2
  17.8 0.0 copy-done
  17.8 0.0 copy-done.3
  17.8 0.0 copy-start.1
  17.9 1.0 copy-done.1
  18.8 0.0 copy-start.4
  18.8 0.7 copy-done.4
  19.5 21.3 %blocks.1 = (f32[12288,128]{1,0:T(8,128)}, f32[8,128]{1,0:T(8,128)S(1)}) custom-call(s32[2048]{0:T(1024)S(1)} %bitcast.7, s32[2048]{0:T(1024)S(1)} %bitcast.6, f32[3,32,64,128]{3,2,1,0:T(8,128)S(1)} %copy-done, f32[6,2,64,128]{3,2,1,0:T(8,128)S(1)} %copy-done.1, bf16[256,256]{1,0:T(8,128)(2,1)S(1)} %copy-done.2), custom_call_target="tpu_custom_call" | custom-call | tf_op jit(solution)/shard_map/blocks/pallas_call | solution.py:314
  40.8 0.0 copy-start.5
  40.8 0.6 copy-done.5
  41.4 143.8 %exchange.1 = (f32[3,8,512,128]{3,2,1,0:T(8,128)}, f32[8,128]{1,0:T(8,128)}) custom-call(f32[3,8,512,128]{3,2,1,0:T(8,128)} %bitcast.8, f32[8,128]{1,0:T(8,128)} %copy-done.5), custom_call_target="tpu_custom_call" | custom-call | tf_op jit(solution)/shard_map/exchange/pallas_call | solution.py:328
  185.2 8.6 %scale.1 = f32[3,8,512,128]{3,2,1,0:T(8,128)} custom-call(s32[1]{0:T(128)} %bitcast.me, f32[8,128]{1,0:T(8,128)} %get-tuple-element.17.squares, f32[3,8,512,128]{3,2,1,0:T(8,128)} %get-tuple-element.18.recv, f32[3,8,512,128]{3,2,1,0:T(8,128)} %bitcast.9), custom_call_target="tpu_custom_call" | custom-call | tf_op jit(solution)/shard_map/scale/pallas_call | solution.py:352
Async XLA Ops:
  0.0 17.8 %copy-start.2 = (bf16[256,256]{1,0:T(8,128)(2,1)S(1)}, bf16[256,256]{1,0:T(8,128)(2,1)}, u32[]{:S(2)}) copy-start(bf16[256,256]{1,0:T(8,128)(2,1)} %constant.15.clone.table) | copy-start | bytes 393220
  0.0 17.8 %copy-start = (f32[3,32,64,128]{3,2,1,0:T(8,128)S(1)}, f32[3,32,64,128]{3,2,1,0:T(8,128)}, u32[]{:S(2)}) copy-start(f32[3,32,64,128]{3,2,1,0:T(8,128)} %vel.5) | copy-start | bytes 9437188
  0.0 17.8 %copy-start.3 = (s32[1,1,1,2048]{3,2,1,0:T(1,128)S(1)}, s32[1,1,1,2048]{3,2,1,0:T(1,128)}, u32[]{:S(2)}) copy-start(s32[1,1,1,2048]{3,2,1,0:T(1,128)} %param.5) | copy-start | bytes 24580
  17.8 1.0 copy-start.1
  18.8 0.7 copy-start.4
  40.8 0.6 copy-start.5

commit v5 on v4

--- a/solution.py
+++ b/solution.py
@@ -10,6 +10,7 @@
 
 BY = 8
 BZ = 16
+UNROLL = 2
 MESH = pl.DeviceIdType.MESH
 
 
@@ -43,7 +44,7 @@
         return tuple(jnp.where(here, new, old) for new, old in zip(rolled, acc))
 
     zero = jnp.zeros((cells_y, cells_z), jnp.float32)
-    columns = lax.fori_loop(0, cells_x, plane, (zero,) * 4)
+    columns = lax.fori_loop(0, cells_x, plane, (zero,) * 4, unroll=4)
     for last in range(2):
         for i in range(2):
             z_faces[last, i] = columns[2 * last + i]
@@ -67,7 +68,7 @@
         rank = inner + jnp.sum(before, axis=1, keepdims=True)
         return jnp.where(mine, w * capacity + rank.astype(jnp.int32), acc)
 
-    slots[...] = lax.fori_loop(0, writers, body, jnp.zeros_like(t))
+    slots[...] = lax.fori_loop(0, writers, body, jnp.zeros_like(t), unroll=8)
 
 
 def halo_kernel(sizes, vel, y_faces, z_faces, halos, send_sem, recv_sem):
@@ -199,13 +200,22 @@
             for spot, cut in found:
                 out[pl.ds(spot, 1), :] = cut
 
-    def step(x, acc):
-        place(x - 1)
-        return plane(x, acc)
-
-    first = plane(0, jnp.zeros((8, cells_z), jnp.float32))
-    squares[...] = lax.fori_loop(1, cells_x, step, first)
-    place(cells_x - 1)
+    together = next(n for n in (UNROLL, 2, 1) if cells_x % n == 0)
+
+    def step(t, acc):
+        for k in range(together):
+            place((t - 1) * together + k)
+        return planes(t, acc)
+
+    def planes(t, acc):
+        for k in range(together):
+            acc = plane(t * together + k, acc)
+        return acc
+
+    first = planes(0, jnp.zeros((8, cells_z), jnp.float32))
+    squares[...] = lax.fori_loop(1, cells_x // together, step, first)
+    for k in range(together):
+        place(cells_x - together + k)
 
 
 def exchange_kernel(

time: 194 us -> 188 us (0.969)
  Pallas kernels: 191 us -> 185 us
    pallas_call x1, Pallas kernels: 21.3 us -> 17.8 us  [local(): pl.pallas_call(blocks_kernel, out_shape=(jax.ShapeDtypeStruct((comps * wr...]
    pallas_call x1, Pallas kernels: 7.57 us -> 4.58 us  [local(): pl.pallas_call(functools.partial(faces_kernel, writers, capacity), out_sh...]
where the time goes in v5:
time: 188 us; the launch traced here: 187 us
  Pallas kernels  185 us (98%)
  local copies, waits for them, and re-layouts  2.29 us (1%)
    pallas_call x1, Pallas kernels, local(): pl.pallas_call(functools.partial(exchange_kernel, n_x, n_y, n_z), out_sha...  144 us
    pallas_call x1, Pallas kernels, local(): pl.pallas_call(blocks_kernel, out_shape=(jax.ShapeDtypeStruct((comps * wr...  17.8 us
    pallas_call x1, Pallas kernels, local(): pl.pallas_call(functools.partial(halo_kernel, (n_x, n_y, n_z)), out_shape...  10.2 us
    pallas_call x1, Pallas kernels, local(): pl.pallas_call(functools.partial(scale_kernel, float(every)), grid_spec=p...  8.57 us
    pallas_call x1, Pallas kernels, local(): pl.pallas_call(functools.partial(faces_kernel, writers, capacity), out_sh...  4.58 us

profile of v5, /device:TPU:0, one launch (start us, length us, event | category | flops | bytes accessed | tf_op | source)
XLA Modules:
  0.0 187.3 jit_solution(17109411906843809271)
XLA Ops:
  0.0 0.0 copy-start.2
  0.0 0.0 copy-start
  0.0 0.0 copy-start.3
  0.0 4.6 %faces.1 = (s32[16,128]{1,0:T(8,128)}, f32[2,2,32,128]{3,2,1,0:T(8,128)}, f32[2,2,64,128]{3,2,1,0:T(8,128)}) custom-call(s32[16,128]{1,0:T(8,128)} %bitcast.10, f32[3,32,64,128]{3,2,1,0:T(8,128)} %vel.5), custom_call_target="tpu_custom_call" | custom-call | tf_op jit(solution)/shard_map/faces/pallas_call | solution.py:304
  4.6 10.2 %halo.1.halos = f32[6,2,64,128]{3,2,1,0:T(8,128)} custom-call(f32[3,32,64,128]{3,2,1,0:T(8,128)} %vel.5, f32[2,2,32,128]{3,2,1,0:T(8,128)} %get-tuple-element.13.y_faces, f32[2,2,64,128]{3,2,1,0:T(8,128)} %get-tuple-element.14.z_faces), custom_call_target="tpu_custom_call" | custom-call | tf_op jit(solution)/shard_map/halo/pallas_call | solution.py:313
  14.8 0.0 copy-done.2
  14.8 0.0 copy-done
  14.8 0.0 copy-done.3
  14.8 0.0 copy-start.1
  14.9 1.0 copy-done.1
  15.8 0.0 copy-start.4
  15.8 0.7 copy-done.4
  16.5 17.8 %blocks.1 = (f32[12288,128]{1,0:T(8,128)}, f32[8,128]{1,0:T(8,128)S(1)}) custom-call(s32[2048]{0:T(1024)S(1)} %bitcast.7, s32[2048]{0:T(1024)S(1)} %bitcast.6, f32[3,32,64,128]{3,2,1,0:T(8,128)S(1)} %copy-done, f32[6,2,64,128]{3,2,1,0:T(8,128)S(1)} %copy-done.1, bf16[256,256]{1,0:T(8,128)(2,1)S(1)} %copy-done.2), custom_call_target="tpu_custom_call" | custom-call | tf_op jit(solution)/shard_map/blocks/pallas_call | solution.py:324
  34.3 0.0 copy-start.5
  34.3 0.6 copy-done.5
  34.9 143.8 %exchange.1 = (f32[3,8,512,128]{3,2,1,0:T(8,128)}, f32[8,128]{1,0:T(8,128)}) custom-call(f32[3,8,512,128]{3,2,1,0:T(8,128)} %bitcast.8, f32[8,128]{1,0:T(8,128)} %copy-done.5), custom_call_target="tpu_custom_call" | custom-call | tf_op jit(solution)/shard_map/exchange/pallas_call | solution.py:338
  178.7 8.6 %scale.1 = f32[3,8,512,128]{3,2,1,0:T(8,128)} custom-call(s32[1]{0:T(128)} %bitcast.me, f32[8,128]{1,0:T(8,128)} %get-tuple-element.17.squares, f32[3,8,512,128]{3,2,1,0:T(8,128)} %get-tuple-element.18.recv, f32[3,8,512,128]{3,2,1,0:T(8,128)} %bitcast.9), custom_call_target="tpu_custom_call" | custom-call | tf_op jit(solution)/shard_map/scale/pallas_call | solution.py:362
Async XLA Ops:
  0.0 14.8 %copy-start.2 = (bf16[256,256]{1,0:T(8,128)(2,1)S(1)}, bf16[256,256]{1,0:T(8,128)(2,1)}, u32[]{:S(2)}) copy-start(bf16[256,256]{1,0:T(8,128)(2,1)} %constant.15.clone.table) | copy-start | bytes 393220
  0.0 14.8 %copy-start = (f32[3,32,64,128]{3,2,1,0:T(8,128)S(1)}, f32[3,32,64,128]{3,2,1,0:T(8,128)}, u32[]{:S(2)}) copy-start(f32[3,32,64,128]{3,2,1,0:T(8,128)} %vel.5) | copy-start | bytes 9437188
  0.0 14.8 %copy-start.3 = (s32[1,1,1,2048]{3,2,1,0:T(1,128)S(1)}, s32[1,1,1,2048]{3,2,1,0:T(1,128)}, u32[]{:S(2)}) copy-start(s32[1,1,1,2048]{3,2,1,0:T(1,128)} %param.5) | copy-start | bytes 24580
  14.8 1.0 copy-start.1
  15.8 0.7 copy-start.4
  34.3 0.6 copy-start.5
